TPU v7x, 32 devices: a whole 2x2x4 slice. The times are simulated.
32 devices in a mesh: ax: 2 (over x), az: 16 (over z, y, core).
Axes of the slice: x: 2, y: 2, z: 4, core: 2. Of those that a mesh axis runs over, the one named last changes fastest.
Arguments:
- state: float32 [4, 8, 128, 2048], P(None, 'ax', 'az'), may hold values from -6 to 6
- rotor_offset: int32 [1], replicated, may hold values from 40 to 87
- rotor_fraction: float32 [1], replicated, may hold values from 0 to 1
Outputs:
- new_state: float32 [4, 8, 128, 2048], P(None, 'ax', 'az')
All inputs are finite; a program needn't handle non-finite values.
Results may differ from a plain program's by a relative error of at most 0.00002.
Values sent between devices are 32-bit elements; how exact they have to be, the bound alone decides.
A program may use at most 64 MiB of HBM per device.

v0:
```python
import functools

import jax
import jax.numpy as jnp
from jax import lax
from jax.experimental import pallas as pl
from jax.experimental.pallas import tpu as pltpu
from jax.sharding import PartitionSpec as P

step_size = 0.2
base_viscosity = 0.05
eddy_coeff = 0.05

LANE = 128
TILE = 256
CHUNK = 256


def kernel(n_ax, n_az, d_min, d_max, off_ref, frac_ref, state, out, q, s, t_send, t_recv, g_send, g_recv0, g_recv1,
           load_sem, ax_send, ax_recv, az_send, az_recv, ag_send, ag_recv):
    nv, planes, cells, radial = state.shape
    half = radial // 2
    wide = half + 2 * LANE
    per_half = half // CHUNK
    count = 2 * per_half
    edge = per_half - 1
    ax = lax.axis_index("ax")
    az = lax.axis_index("az")
    has_up = ax < n_ax - 1
    has_dn = ax > 0
    nxt = lax.rem(az + 1, n_az)
    prv = lax.rem(az + n_az - 1, n_az)
    reach = d_max - d_min + 1
    g_recv = (g_recv0, g_recv1)

    loads = [
        pltpu.make_async_copy(
            state.at[:, :, :, pl.ds(h * half, half)],
            q.at[:, pl.ds(1, planes), :, pl.ds(h * wide + LANE, half)],
            load_sem.at[h],
        )
        for h in range(2)
    ]
    for load in loads:
        load.start()

    barrier = pltpu.get_barrier_semaphore()

    @pl.when(has_up)
    def _():
        pl.semaphore_signal(barrier, inc=1, device_id={"ax": ax + 1})

    @pl.when(has_dn)
    def _():
        pl.semaphore_signal(barrier, inc=1, device_id={"ax": ax - 1})

    for d in [1, n_az - 1] + list(range(d_min, d_max + 1)):
        pl.semaphore_signal(barrier, inc=1, device_id={"az": lax.rem(az + d, n_az)})

    zero = jnp.zeros((cells, LANE), jnp.float32)
    for field in (q, s):
        for v in range(nv):
            for p in range(planes):
                field[v, p + 1, :, 0:LANE] = zero
                field[v, p + 1, :, 2 * wide - LANE :] = zero

        @pl.when(jnp.logical_not(has_dn))
        def _(field=field):
            for v in range(nv):
                field[v, 0, :, :] = jnp.zeros((cells, 2 * wide), jnp.float32)

        @pl.when(jnp.logical_not(has_up))
        def _(field=field):
            for v in range(nv):
                field[v, planes + 1, :, :] = jnp.zeros((cells, 2 * wide), jnp.float32)

    sub = lax.broadcasted_iota(jnp.int32, (cells, TILE), 0)
    sub1 = lax.broadcasted_iota(jnp.int32, (cells, LANE), 0)
    lane1 = lax.broadcasted_iota(jnp.int32, (cells, LANE), 1)

    for load in loads:
        load.wait()

    def axial(field, turn, index, up):
        h, c = index // per_half, index % per_half
        lanes = pl.ds(pl.multiple_of(h * wide + LANE + c * CHUNK, LANE), CHUNK)
        way = 0 if up else 1
        return pltpu.make_async_remote_copy(
            src_ref=field.at[:, planes if up else 1, :, lanes],
            dst_ref=field.at[:, 0 if up else planes + 1, :, lanes],
            send_sem=ax_send.at[turn, way, index],
            recv_sem=ax_recv.at[turn, way, index],
            device_id={"ax": ax + 1 if up else ax - 1},
        )

    def axial_start(field, turn, index):
        @pl.when(has_up)
        def _():
            axial(field, turn, index, True).start()

        @pl.when(has_dn)
        def _():
            axial(field, turn, index, False).start()

    def axial_wait(field, turn, index):
        @pl.when(has_dn)
        def _():
            axial(field, turn, index, True).wait_recv()

        @pl.when(has_up)
        def _():
            axial(field, turn, index, False).wait_recv()

    def axial_drain(field, turn, index):
        @pl.when(has_up)
        def _():
            axial(field, turn, index, True).wait_send()

        @pl.when(has_dn)
        def _():
            axial(field, turn, index, False).wait_send()

    def sector(turn, way, part):
        where = (slice(None), slice(None), slice(None), pl.ds(pl.multiple_of(part * CHUNK, LANE), CHUNK))
        return pltpu.make_async_remote_copy(
            src_ref=t_send.at[(turn, way) + where],
            dst_ref=t_recv.at[(turn, way) + where],
            send_sem=az_send.at[turn, way, part],
            recv_sem=az_recv.at[turn, way, part],
            device_id={"az": nxt if way == 0 else prv},
        )

    def spread(turn, d):
        return pltpu.make_async_remote_copy(
            src_ref=g_send.at[turn],
            dst_ref=g_recv[turn].at[d - d_min],
            send_sem=ag_send.at[turn, d - d_min],
            recv_sem=ag_recv.at[turn, d - d_min],
            device_id={"az": lax.rem(az + d, n_az)},
        )

    def pack_layers(field, turn):
        packed = zero
        for v in range(nv):
            for p in range(planes):
                index = v * planes + p
                stator = field[v, p + 1, :, wide + LANE : wide + 2 * LANE]
                rotor = field[v, p + 1, :, wide - 2 * LANE : wide - LANE]
                other = nv * planes + index
                if index:
                    stator = pltpu.roll(stator, index, 1)
                packed = jnp.where(lane1 == index, stator, packed)
                packed = jnp.where(lane1 == other, pltpu.roll(rotor, other + 1, 1), packed)
        g_send[turn] = packed

    def unpack_ghosts(field, turn):
        off = off_ref[0]
        f = frac_ref[0]

        def window(a, b, shift):
            turned = lax.rem(2 * cells - shift, cells)
            return jnp.where(sub1 < cells - shift, pltpu.roll(a, turned, 0), pltpu.roll(b, turned, 0))

        def between(start, lo, hi):
            k = jnp.clip(lax.div(start, cells), d_min, d_max - 1)
            r = lax.rem(start, cells)
            a = g_recv[turn][n_az - k - d_min]
            b = g_recv[turn][n_az - k - 1 - d_min]
            return lo * window(a, b, r) + hi * window(a, b, r + 1)

        rot = between(off, 1.0 - f, f)
        sta = between(n_az * cells - off - 1, f, 1.0 - f)
        for v in range(nv):
            for p in range(planes):
                index = v * planes + p
                other = nv * planes + index
                field[v, p + 1, :, wide - LANE : wide] = pltpu.roll(rot, LANE - index, 1) if index else rot
                field[v, p + 1, :, wide : wide + LANE] = pltpu.roll(sta, LANE - 1 - other, 1)

    def evaluate(field, turn, p, slot, base, tbase):
        values, grads, seconds = [], [], []
        strain = None
        for v in range(nv):
            ext = field[v, p + 1, :, pl.ds(base, TILE + 2 * LANE)]
            value = ext[:, LANE : LANE + TILE]
            up_r = pltpu.roll(ext, TILE + 2 * LANE - 1, 1)[:, LANE : LANE + TILE]
            dn_r = pltpu.roll(ext, 1, 1)[:, LANE : LANE + TILE]
            up_p = field[v, p + 2, :, pl.ds(base + LANE, TILE)]
            dn_p = field[v, p, :, pl.ds(base + LANE, TILE)]
            before = t_recv[turn, 0, slot, v, :, pl.ds(tbase, TILE)]
            after = t_recv[turn, 1, slot, v, :, pl.ds(tbase, TILE)]
            up_t = pltpu.roll(jnp.where(sub == 0, after, value), cells - 1, 0)
            dn_t = pltpu.roll(jnp.where(sub == cells - 1, before, value), 1, 0)
            grad = ((up_p - dn_p) * 0.5, (up_t - dn_t) * 0.5, (up_r - dn_r) * 0.5)
            second = (up_p + dn_p) + (up_t + dn_t) + (up_r + dn_r) - 6.0 * value
            if v < 3:
                square = grad[0] * grad[0] + grad[1] * grad[1] + grad[2] * grad[2]
                strain = square if strain is None else strain + square
            values.append(value)
            grads.append(grad)
            seconds.append(second)
        viscous = base_viscosity + eddy_coeff * jnp.sqrt(strain)
        steps = []
        for v in range(nv):
            advect = values[0] * grads[v][0] + values[1] * grads[v][1] + values[2] * grads[v][2]
            steps.append(step_size * (viscous * seconds[v] - advect))
        return values, steps

    def first(p, slot, base, tbase):
        values, steps = evaluate(q, 0, p, slot, base, tbase)
        for v in range(nv):
            section = values[v] + steps[v]
            s[v, p + 1, :, pl.ds(base + LANE, TILE)] = section
            t_send[1, 0, slot, v, :, pl.ds(tbase, TILE)] = section[cells - 1 :, :]
            t_send[1, 1, slot, v, :, pl.ds(tbase, TILE)] = section[0:1, :]

    def second(p, slot, base, tbase):
        values, steps = evaluate(s, 1, p, slot, base, tbase)
        for v in range(nv):
            before = q[v, p + 1, :, pl.ds(base + LANE, TILE)]
            out[v, p, :, pl.ds(tbase, TILE)] = 0.5 * (before + (values[v] + steps[v]))

    def evaluate_chunk(work, index):
        h, c = index // per_half, index % per_half
        base = pl.multiple_of(h * wide + c * CHUNK, LANE)
        tbase = pl.multiple_of(index * CHUNK, LANE)
        for p in range(planes):
            work(p, p, base, tbase)

    parts = range(count)
    pack_layers(q, 0)
    for slot in range(planes):
        p = slot
        for v in range(nv):
            for h in range(2):
                lanes = slice(h * wide + LANE, h * wide + LANE + half)
                t_send[0, 0, slot, v, :, h * half : (h + 1) * half] = q[v, p + 1, cells - 1 : cells, lanes]
                t_send[0, 1, slot, v, :, h * half : (h + 1) * half] = q[v, p + 1, 0:1, lanes]

    neighbours = has_up.astype(jnp.int32) + has_dn.astype(jnp.int32)
    pl.semaphore_wait(barrier, neighbours + 2 + reach)

    order = [edge, edge + 1] + list(range(edge)) + list(range(edge + 2, count))
    for index in order:
        axial_start(q, 0, index)
    for d in range(d_min, d_max + 1):
        spread(0, d).start()
    for index in order:
        for way in range(2):
            sector(0, way, index).start()

    def run_first(low, high):
        @pl.loop(low, high)
        def _(index):
            for way in range(2):
                sector(0, way, index).wait_recv()
            axial_wait(q, 0, index)
            evaluate_chunk(first, index)
            axial_start(s, 1, index)
            for way in range(2):
                sector(1, way, index).start()

    def run_second(low, high):
        @pl.loop(low, high)
        def _(index):
            for way in range(2):
                sector(1, way, index).wait_recv()
            axial_wait(s, 1, index)
            evaluate_chunk(second, index)

    for d in range(d_min, d_max + 1):
        spread(0, d).wait_recv()
    unpack_ghosts(q, 0)
    run_first(edge, edge + 2)
    pack_layers(s, 1)
    for d in range(d_min, d_max + 1):
        spread(1, d).start()
    run_first(0, edge)
    run_first(edge + 2, count)

    run_second(0, edge)
    for d in range(d_min, d_max + 1):
        spread(1, d).wait_recv()
    unpack_ghosts(s, 1)
    run_second(edge, edge + 2)
    run_second(edge + 2, count)

    for turn, field in ((0, q), (1, s)):
        for d in range(d_min, d_max + 1):
            spread(turn, d).wait_send()
        for part in parts:
            for way in range(2):
                sector(turn, way, part).wait_send()
        for index in range(count):
            axial_drain(field, turn, index)


def shards(n_ax, n_az, state, rotor_offset, rotor_fraction):
    nv, planes, cells, radial = state.shape
    around = n_az * cells
    low, high = around // 4 + cells, 3 * around // 4 - cells - 1
    d_min, d_max = low // cells, high // cells + 1
    reach = d_max - d_min + 1
    wide = radial // 2 + 2 * LANE
    count = radial // CHUNK
    sem = pltpu.SemaphoreType.DMA
    return pl.pallas_call(
        functools.partial(kernel, n_ax, n_az, d_min, d_max),
        out_shape=jax.ShapeDtypeStruct(state.shape, state.dtype),
        in_specs=[
            pl.BlockSpec(memory_space=pltpu.SMEM),
            pl.BlockSpec(memory_space=pltpu.SMEM),
            pl.BlockSpec(memory_space=pltpu.HBM),
        ],
        out_specs=pl.BlockSpec(memory_space=pltpu.VMEM),
        scratch_shapes=[
            pltpu.VMEM((nv, planes + 2, cells, 2 * wide), jnp.float32),
            pltpu.VMEM((nv, planes + 2, cells, 2 * wide), jnp.float32),
            pltpu.VMEM((2, 2, planes, nv, 1, radial), jnp.float32),
            pltpu.VMEM((2, 2, planes, nv, 1, radial), jnp.float32),
            pltpu.VMEM((2, cells, LANE), jnp.float32),
            pltpu.VMEM((reach, cells, LANE), jnp.float32),
            pltpu.VMEM((reach, cells, LANE), jnp.float32),
            sem((2,)),
            sem((2, 2, count)),
            sem((2, 2, count)),
            sem((2, 2, count)),
            sem((2, 2, count)),
            sem((2, reach)),
            sem((2, reach)),
        ],
        compiler_params=pltpu.CompilerParams(collective_id=0, has_side_effects=True, vmem_limit_bytes=55_000_000),
    )(rotor_offset, rotor_fraction, state)


def solution(mesh):
    return jax.shard_map(
        functools.partial(shards, mesh.shape["ax"], mesh.shape["az"]),
        mesh=mesh,
        in_specs=(P(None, "ax", "az", None), P(), P()),
        out_specs=P(None, "ax", "az", None),
        check_vma=False,
    )
```

profile of v0, /device:TPU:0, one launch (start us, length us, event | category | flops | bytes accessed | tf_op | source)
XLA Modules:
  0.0 22.9 jit_solution(1125933943512349542)
XLA Ops:
  1.3 20.6 %shard_map.37 = f32[4,4,8,2048]{3,2,1,0:T(8,128)S(1)} custom-call(s32[1]{0:T(128)S(6)} %copy.5.off_ref, f32[1]{0:T(128)S(6)} %copy.6.frac_ref, f32[4,4,8,2048]{3,2,1,0:T(8,128)} %state.1), custom_call_target="tpu_custom_call" | custom-call | tf_op jit(solution)/shard_map/pallas_call | solution.py:307
  21.9 1.0 %copy.7 = f32[4,4,8,2048]{3,2,1,0:T(8,128)} copy(f32[4,4,8,2048]{3,2,1,0:T(8,128)S(1)} %shard_map.37) | data formatting | bytes 2097152
where the time goes:
time: 23.1 us; the launch traced here: 22.9 us
  Pallas kernels  20.6 us (89%)
  between operations  1.3 us (6%)
  local copies, waits for them, and re-layouts  0.97 us (4%)
    pallas_call x1, Pallas kernels, shards(): pl.pallas_call(functools.partial(kernel, n_ax, n_az, d_min, d_max), out_s...  20.6 us
    unnamed x1, local copies, waits for them, and re-layouts  0.97 us

commit v1 on v0

--- a/solution.py
+++ b/solution.py
@@ -16,8 +16,8 @@
 CHUNK = 256
 
 
-def kernel(n_ax, n_az, d_min, d_max, off_ref, frac_ref, state, out, q, s, t_send, t_recv, g_send, g_recv0, g_recv1,
-           load_sem, ax_send, ax_recv, az_send, az_recv, ag_send, ag_recv):
+def kernel(n_ax, n_az, d_min, d_max, off_hbm, frac_hbm, state, out, q, s, t_send, t_recv, g_send, g_recv0, g_recv1,
+           off_ref, frac_ref, load_sem, ax_send, ax_recv, az_send, az_recv, ag_send, ag_recv, ready):
     nv, planes, cells, radial = state.shape
     half = radial // 2
     wide = half + 2 * LANE
@@ -41,10 +41,18 @@
         )
         for h in range(2)
     ]
-    for load in loads:
+    scalars = [
+        pltpu.make_async_copy(off_hbm, off_ref, load_sem.at[2]),
+        pltpu.make_async_copy(frac_hbm, frac_ref, load_sem.at[3]),
+    ]
+    for load in loads + scalars:
         load.start()
 
     barrier = pltpu.get_barrier_semaphore()
+    peers = [1, n_az - 1] + list(range(d_min, d_max + 1))
+
+    def early(sector):
+        return jnp.logical_and(lax.rem(sector, 2) == 0, sector < d_min)
 
     @pl.when(has_up)
     def _():
@@ -54,8 +62,12 @@
     def _():
         pl.semaphore_signal(barrier, inc=1, device_id={"ax": ax - 1})
 
-    for d in [1, n_az - 1] + list(range(d_min, d_max + 1)):
-        pl.semaphore_signal(barrier, inc=1, device_id={"az": lax.rem(az + d, n_az)})
+    for d in peers:
+        peer = lax.rem(az + d, n_az)
+
+        @pl.when(jnp.logical_not(early(peer)))
+        def _(peer=peer):
+            pl.semaphore_signal(barrier, inc=1, device_id={"az": peer})
 
     zero = jnp.zeros((cells, LANE), jnp.float32)
     for field in (q, s):
@@ -238,11 +250,23 @@
                 t_send[0, 1, slot, v, :, h * half : (h + 1) * half] = q[v, p + 1, 0:1, lanes]
 
     neighbours = has_up.astype(jnp.int32) + has_dn.astype(jnp.int32)
-    pl.semaphore_wait(barrier, neighbours + 2 + reach)
+    pl.semaphore_wait(barrier, neighbours + jnp.where(early(az), 0, 2 + reach))
 
     order = [edge, edge + 1] + list(range(edge)) + list(range(edge + 2, count))
     for index in order:
         axial_start(q, 0, index)
+
+    for d in peers:
+        peer = lax.rem(az + d, n_az)
+
+        @pl.when(early(peer))
+        def _(peer=peer):
+            pl.semaphore_signal(ready, inc=1, device_id={"az": peer})
+
+    @pl.when(early(az))
+    def _():
+        pl.semaphore_wait(ready, 2 + reach)
+
     for d in range(d_min, d_max + 1):
         spread(0, d).start()
     for index in order:
@@ -270,6 +294,8 @@
 
     for d in range(d_min, d_max + 1):
         spread(0, d).wait_recv()
+    for scalar in scalars:
+        scalar.wait()
     unpack_ghosts(q, 0)
     run_first(edge, edge + 2)
     pack_layers(s, 1)
@@ -308,8 +334,8 @@
         functools.partial(kernel, n_ax, n_az, d_min, d_max),
         out_shape=jax.ShapeDtypeStruct(state.shape, state.dtype),
         in_specs=[
-            pl.BlockSpec(memory_space=pltpu.SMEM),
-            pl.BlockSpec(memory_space=pltpu.SMEM),
+            pl.BlockSpec(memory_space=pltpu.HBM),
+            pl.BlockSpec(memory_space=pltpu.HBM),
             pl.BlockSpec(memory_space=pltpu.HBM),
         ],
         out_specs=pl.BlockSpec(memory_space=pltpu.VMEM),
@@ -321,13 +347,16 @@
             pltpu.VMEM((2, cells, LANE), jnp.float32),
             pltpu.VMEM((reach, cells, LANE), jnp.float32),
             pltpu.VMEM((reach, cells, LANE), jnp.float32),
-            sem((2,)),
+            pltpu.SMEM((1,), jnp.int32),
+            pltpu.SMEM((1,), jnp.float32),
+            sem((4,)),
             sem((2, 2, count)),
             sem((2, 2, count)),
             sem((2, 2, count)),
             sem((2, 2, count)),
             sem((2, reach)),
             sem((2, reach)),
+            pltpu.SemaphoreType.REGULAR,
         ],
         compiler_params=pltpu.CompilerParams(collective_id=0, has_side_effects=True, vmem_limit_bytes=55_000_000),
     )(rotor_offset, rotor_fraction, state)

time: 23.1 us -> 21.7 us (0.939)
  Pallas kernels: 20.6 us -> 19.2 us
    pallas_call x1, Pallas kernels: 20.6 us -> 19.2 us  [shards(): pl.pallas_call(functools.partial(kernel, n_ax, n_az, d_min, d_max), out_s...]
where the time goes in v1:
time: 21.7 us; the launch traced here: 21.5 us
  Pallas kernels  19.2 us (88%)
  between operations  1.3 us (6%)
  local copies, waits for them, and re-layouts  0.97 us (4%)
    pallas_call x1, Pallas kernels, shards(): pl.pallas_call(functools.partial(kernel, n_ax, n_az, d_min, d_max), out_s...  19.2 us
    unnamed x1, local copies, waits for them, and re-layouts  0.97 us

profile of v1, /device:TPU:0, one launch (start us, length us, event | category | flops | bytes accessed | tf_op | source)
XLA Modules:
  0.0 21.5 jit_solution(9474766059934464220)
XLA Ops:
  1.3 19.2 %shard_map.37 = f32[4,4,8,2048]{3,2,1,0:T(8,128)S(1)} custom-call(s32[1]{0:T(128)S(6)} %copy.5.off_hbm, f32[1]{0:T(128)S(6)} %copy.6.frac_hbm, f32[4,4,8,2048]{3,2,1,0:T(8,128)} %state.1), custom_call_target="tpu_custom_call" | custom-call | tf_op jit(solution)/shard_map/pallas_call | solution.py:333
  20.5 1.0 %copy.7 = f32[4,4,8,2048]{3,2,1,0:T(8,128)} copy(f32[4,4,8,2048]{3,2,1,0:T(8,128)S(1)} %shard_map.37) | data formatting | bytes 2097152

commit v2 on v0

--- a/solution.py
+++ b/solution.py
@@ -16,8 +16,8 @@
 CHUNK = 256
 
 
-def kernel(n_ax, n_az, d_min, d_max, off_ref, frac_ref, state, out, q, s, t_send, t_recv, g_send, g_recv0, g_recv1,
-           load_sem, ax_send, ax_recv, az_send, az_recv, ag_send, ag_recv):
+def kernel(n_ax, n_az, d_min, d_max, off_hbm, frac_hbm, state, out, q, s, t_send, t_recv, g_send, g_recv0, g_recv1,
+           off_ref, frac_ref, load_sem, ax_send, ax_recv, az_send, az_recv, ag_send, ag_recv, ready):
     nv, planes, cells, radial = state.shape
     half = radial // 2
     wide = half + 2 * LANE
@@ -30,19 +30,23 @@
     has_dn = ax > 0
     nxt = lax.rem(az + 1, n_az)
     prv = lax.rem(az + n_az - 1, n_az)
-    reach = d_max - d_min + 1
     g_recv = (g_recv0, g_recv1)
 
-    loads = [
-        pltpu.make_async_copy(
-            state.at[:, :, :, pl.ds(h * half, half)],
-            q.at[:, pl.ds(1, planes), :, pl.ds(h * wide + LANE, half)],
-            load_sem.at[h],
+    def load(first, number, h, slot):
+        return pltpu.make_async_copy(
+            state.at[:, pl.ds(first, number), :, pl.ds(h * half, half)],
+            q.at[:, pl.ds(first + 1, number), :, pl.ds(h * wide + LANE, half)],
+            load_sem.at[slot, h],
         )
-        for h in range(2)
+
+    outer_loads = [load(p, 1, h, i) for i, p in enumerate((0, planes - 1)) for h in range(2)]
+    inner_loads = [load(1, planes - 2, h, 2) for h in range(2)]
+    scalars = [
+        pltpu.make_async_copy(off_hbm, off_ref, load_sem.at[3, 0]),
+        pltpu.make_async_copy(frac_hbm, frac_ref, load_sem.at[3, 1]),
     ]
-    for load in loads:
-        load.start()
+    for copy in outer_loads + inner_loads + scalars:
+        copy.start()
 
     barrier = pltpu.get_barrier_semaphore()
 
@@ -54,32 +58,28 @@
     def _():
         pl.semaphore_signal(barrier, inc=1, device_id={"ax": ax - 1})
 
-    for d in [1, n_az - 1] + list(range(d_min, d_max + 1)):
-        pl.semaphore_signal(barrier, inc=1, device_id={"az": lax.rem(az + d, n_az)})
+    layer_peers = list(range(d_min, d_max + 1))
+
+    def sector_at(d):
+        return lax.rem(az + d, n_az)
+
+    def before(d):
+        return sector_at(d) < az
+
+    def number_before(ds):
+        return sum(before(d).astype(jnp.int32) for d in ds)
+
+    for d in [1, n_az - 1] + layer_peers:
+
+        @pl.when(jnp.logical_not(before(d)))
+        def _(d=d):
+            pl.semaphore_signal(barrier, inc=1, device_id={"az": sector_at(d)})
 
     zero = jnp.zeros((cells, LANE), jnp.float32)
-    for field in (q, s):
-        for v in range(nv):
-            for p in range(planes):
-                field[v, p + 1, :, 0:LANE] = zero
-                field[v, p + 1, :, 2 * wide - LANE :] = zero
-
-        @pl.when(jnp.logical_not(has_dn))
-        def _(field=field):
-            for v in range(nv):
-                field[v, 0, :, :] = jnp.zeros((cells, 2 * wide), jnp.float32)
-
-        @pl.when(jnp.logical_not(has_up))
-        def _(field=field):
-            for v in range(nv):
-                field[v, planes + 1, :, :] = jnp.zeros((cells, 2 * wide), jnp.float32)
 
     sub = lax.broadcasted_iota(jnp.int32, (cells, TILE), 0)
     sub1 = lax.broadcasted_iota(jnp.int32, (cells, LANE), 0)
     lane1 = lax.broadcasted_iota(jnp.int32, (cells, LANE), 1)
-
-    for load in loads:
-        load.wait()
 
     def axial(field, turn, index, up):
         h, c = index // per_half, index % per_half
@@ -220,15 +220,30 @@
             before = q[v, p + 1, :, pl.ds(base + LANE, TILE)]
             out[v, p, :, pl.ds(tbase, TILE)] = 0.5 * (before + (values[v] + steps[v]))
 
-    def evaluate_chunk(work, index):
+    def evaluate_chunk(work, index, which):
         h, c = index // per_half, index % per_half
         base = pl.multiple_of(h * wide + c * CHUNK, LANE)
         tbase = pl.multiple_of(index * CHUNK, LANE)
-        for p in range(planes):
+        for p in which:
             work(p, p, base, tbase)
 
+    neighbours = has_up.astype(jnp.int32) + has_dn.astype(jnp.int32)
+    pl.semaphore_wait(barrier, neighbours + number_before([1, n_az - 1] + layer_peers))
+    for d, slot in [(n_az - 1, 0), (1, 1)] + [(d, 2) for d in layer_peers]:
+
+        @pl.when(before(d))
+        def _(d=d, slot=slot):
+            pl.semaphore_signal(ready.at[slot], inc=1, device_id={"az": sector_at(d)})
+
+    for copy in outer_loads:
+        copy.wait()
     parts = range(count)
-    pack_layers(q, 0)
+    order = [edge, edge + 1] + list(range(edge)) + list(range(edge + 2, count))
+    for index in order:
+        axial_start(q, 0, index)
+
+    for copy in inner_loads:
+        copy.wait()
     for slot in range(planes):
         p = slot
         for v in range(nv):
@@ -237,17 +252,62 @@
                 t_send[0, 0, slot, v, :, h * half : (h + 1) * half] = q[v, p + 1, cells - 1 : cells, lanes]
                 t_send[0, 1, slot, v, :, h * half : (h + 1) * half] = q[v, p + 1, 0:1, lanes]
 
-    neighbours = has_up.astype(jnp.int32) + has_dn.astype(jnp.int32)
-    pl.semaphore_wait(barrier, neighbours + 2 + reach)
-
-    order = [edge, edge + 1] + list(range(edge)) + list(range(edge + 2, count))
-    for index in order:
-        axial_start(q, 0, index)
-    for d in range(d_min, d_max + 1):
-        spread(0, d).start()
-    for index in order:
-        for way in range(2):
+    def sector_start(way):
+        for index in order:
             sector(0, way, index).start()
+
+    @pl.when(before(n_az - 1))
+    def _():
+        sector_start(1)
+
+    @pl.when(before(1))
+    def _():
+        sector_start(0)
+
+    pack_layers(q, 0)
+    for d in layer_peers:
+
+        @pl.when(before(d))
+        def _(d=d):
+            spread(0, d).start()
+
+    @pl.when(jnp.logical_not(before(1)))
+    def _():
+        pl.semaphore_wait(ready.at[0], 1)
+        sector_start(0)
+
+    for field in (q, s):
+        for v in range(nv):
+            for p in range(planes):
+                field[v, p + 1, :, 0:LANE] = zero
+                field[v, p + 1, :, 2 * wide - LANE :] = zero
+
+        @pl.when(jnp.logical_not(has_dn))
+        def _(field=field):
+            for v in range(nv):
+                field[v, 0, :, :] = jnp.zeros((cells, 2 * wide), jnp.float32)
+
+        @pl.when(jnp.logical_not(has_up))
+        def _(field=field):
+            for v in range(nv):
+                field[v, planes + 1, :, :] = jnp.zeros((cells, 2 * wide), jnp.float32)
+
+    @pl.when(jnp.logical_not(before(n_az - 1)))
+    def _():
+        pl.semaphore_wait(ready.at[1], 1)
+        sector_start(1)
+
+    after = len(layer_peers) - number_before(layer_peers)
+
+    @pl.when(after > 0)
+    def _():
+        pl.semaphore_wait(ready.at[2], after)
+
+    for d in layer_peers:
+
+        @pl.when(jnp.logical_not(before(d)))
+        def _(d=d):
+            spread(0, d).start()
 
     def run_first(low, high):
         @pl.loop(low, high)
@@ -255,7 +315,7 @@
             for way in range(2):
                 sector(0, way, index).wait_recv()
             axial_wait(q, 0, index)
-            evaluate_chunk(first, index)
+            evaluate_chunk(first, index, range(planes))
             axial_start(s, 1, index)
             for way in range(2):
                 sector(1, way, index).start()
@@ -265,11 +325,14 @@
         def _(index):
             for way in range(2):
                 sector(1, way, index).wait_recv()
+            evaluate_chunk(second, index, range(1, planes - 1))
             axial_wait(s, 1, index)
-            evaluate_chunk(second, index)
+            evaluate_chunk(second, index, (0, planes - 1))
 
     for d in range(d_min, d_max + 1):
         spread(0, d).wait_recv()
+    for scalar in scalars:
+        scalar.wait()
     unpack_ghosts(q, 0)
     run_first(edge, edge + 2)
     pack_layers(s, 1)
@@ -279,11 +342,12 @@
     run_first(edge + 2, count)
 
     run_second(0, edge)
+    run_second(edge + 2, count - 1)
     for d in range(d_min, d_max + 1):
         spread(1, d).wait_recv()
     unpack_ghosts(s, 1)
     run_second(edge, edge + 2)
-    run_second(edge + 2, count)
+    run_second(count - 1, count)
 
     for turn, field in ((0, q), (1, s)):
         for d in range(d_min, d_max + 1):
@@ -308,8 +372,8 @@
         functools.partial(kernel, n_ax, n_az, d_min, d_max),
         out_shape=jax.ShapeDtypeStruct(state.shape, state.dtype),
         in_specs=[
-            pl.BlockSpec(memory_space=pltpu.SMEM),
-            pl.BlockSpec(memory_space=pltpu.SMEM),
+            pl.BlockSpec(memory_space=pltpu.HBM),
+            pl.BlockSpec(memory_space=pltpu.HBM),
             pl.BlockSpec(memory_space=pltpu.HBM),
         ],
         out_specs=pl.BlockSpec(memory_space=pltpu.VMEM),
@@ -321,13 +385,16 @@
             pltpu.VMEM((2, cells, LANE), jnp.float32),
             pltpu.VMEM((reach, cells, LANE), jnp.float32),
             pltpu.VMEM((reach, cells, LANE), jnp.float32),
-            sem((2,)),
+            pltpu.SMEM((1,), jnp.int32),
+            pltpu.SMEM((1,), jnp.float32),
+            sem((4, 2)),
             sem((2, 2, count)),
             sem((2, 2, count)),
             sem((2, 2, count)),
             sem((2, 2, count)),
             sem((2, reach)),
             sem((2, reach)),
+            pltpu.SemaphoreType.REGULAR((3,)),
         ],
         compiler_params=pltpu.CompilerParams(collective_id=0, has_side_effects=True, vmem_limit_bytes=55_000_000),
     )(rotor_offset, rotor_fraction, state)

time: 23.1 us -> 23.7 us (1.026)
  Pallas kernels: 20.6 us -> 21.2 us
    pallas_call x1, Pallas kernels: 20.6 us -> 21.2 us  [shards(): pl.pallas_call(functools.partial(kernel, n_ax, n_az, d_min, d_max), out_s...]
where the time goes in v2:
time: 23.7 us; the launch traced here: 23.5 us
  Pallas kernels  21.2 us (89%)
  between operations  1.3 us (5%)
  local copies, waits for them, and re-layouts  0.97 us (4%)
    pallas_call x1, Pallas kernels, shards(): pl.pallas_call(functools.partial(kernel, n_ax, n_az, d_min, d_max), out_s...  21.2 us
    unnamed x1, local copies, waits for them, and re-layouts  0.97 us

profile of v2, /device:TPU:0, one launch (start us, length us, event | category | flops | bytes accessed | tf_op | source)
XLA Modules:
  0.0 23.5 jit_solution(8039354737122842318)
XLA Ops:
  1.3 21.2 %shard_map.37 = f32[4,4,8,2048]{3,2,1,0:T(8,128)S(1)} custom-call(s32[1]{0:T(128)S(6)} %copy.5.off_hbm, f32[1]{0:T(128)S(6)} %copy.6.frac_hbm, f32[4,4,8,2048]{3,2,1,0:T(8,128)} %state.1), custom_call_target="tpu_custom_call" | custom-call | tf_op jit(solution)/shard_map/pallas_call | solution.py:371
  22.5 1.0 %copy.7 = f32[4,4,8,2048]{3,2,1,0:T(8,128)} copy(f32[4,4,8,2048]{3,2,1,0:T(8,128)S(1)} %shard_map.37) | data formatting | bytes 2097152

commit v3 on v2

--- a/solution.py
+++ b/solution.py
@@ -24,41 +24,42 @@
     per_half = half // CHUNK
     count = 2 * per_half
     edge = per_half - 1
+    g_recv = (g_recv0, g_recv1)
     ax = lax.axis_index("ax")
     az = lax.axis_index("az")
     has_up = ax < n_ax - 1
     has_dn = ax > 0
     nxt = lax.rem(az + 1, n_az)
     prv = lax.rem(az + n_az - 1, n_az)
-    g_recv = (g_recv0, g_recv1)
 
     def load(first, number, h, slot):
         return pltpu.make_async_copy(
             state.at[:, pl.ds(first, number), :, pl.ds(h * half, half)],
             q.at[:, pl.ds(first + 1, number), :, pl.ds(h * wide + LANE, half)],
-            load_sem.at[slot, h],
+            load_sem.at[slot],
         )
 
-    outer_loads = [load(p, 1, h, i) for i, p in enumerate((0, planes - 1)) for h in range(2)]
-    inner_loads = [load(1, planes - 2, h, 2) for h in range(2)]
+    outer_loads = [load(p, 1, h, 0) for p in (0, planes - 1) for h in range(2)]
+    inner_loads = [load(1, planes - 2, h, 1) for h in range(2)]
     scalars = [
-        pltpu.make_async_copy(off_hbm, off_ref, load_sem.at[3, 0]),
-        pltpu.make_async_copy(frac_hbm, frac_ref, load_sem.at[3, 1]),
+        pltpu.make_async_copy(off_hbm, off_ref, load_sem.at[2]),
+        pltpu.make_async_copy(frac_hbm, frac_ref, load_sem.at[3]),
     ]
     for copy in outer_loads + inner_loads + scalars:
         copy.start()
 
+    def all_of(ref, semaphore):
+        pltpu.make_async_copy(ref, ref, semaphore).wait()
+
+    def loaded(number, slot):
+        all_of(out.at[:, pl.ds(0, number)], load_sem.at[slot])
+
     barrier = pltpu.get_barrier_semaphore()
 
-    @pl.when(has_up)
-    def _():
-        pl.semaphore_signal(barrier, inc=1, device_id={"ax": ax + 1})
-
-    @pl.when(has_dn)
-    def _():
-        pl.semaphore_signal(barrier, inc=1, device_id={"ax": ax - 1})
-
     layer_peers = list(range(d_min, d_max + 1))
+    even = lax.rem(ax, 2) == 0
+    first_even = jnp.logical_and(az == 0, even)
+    first_odd = jnp.logical_and(az == 0, jnp.logical_not(even))
 
     def sector_at(d):
         return lax.rem(az + d, n_az)
@@ -69,9 +70,22 @@
     def number_before(ds):
         return sum(before(d).astype(jnp.int32) for d in ds)
 
+    def direct(d):
+        return jnp.logical_and(jnp.logical_and(sector_at(d) == 0, even), d != n_az - 1)
+
+    def signal_axial(semaphore, when):
+        @pl.when(jnp.logical_and(when, has_up))
+        def _():
+            pl.semaphore_signal(semaphore, inc=1, device_id={"ax": ax + 1})
+
+        @pl.when(jnp.logical_and(when, has_dn))
+        def _():
+            pl.semaphore_signal(semaphore, inc=1, device_id={"ax": ax - 1})
+
+    signal_axial(barrier, jnp.logical_not(first_odd))
     for d in [1, n_az - 1] + layer_peers:
 
-        @pl.when(jnp.logical_not(before(d)))
+        @pl.when(jnp.logical_or(jnp.logical_not(before(d)), direct(d)))
         def _(d=d):
             pl.semaphore_signal(barrier, inc=1, device_id={"az": sector_at(d)})
 
@@ -88,8 +102,8 @@
         return pltpu.make_async_remote_copy(
             src_ref=field.at[:, planes if up else 1, :, lanes],
             dst_ref=field.at[:, 0 if up else planes + 1, :, lanes],
-            send_sem=ax_send.at[turn, way, index],
-            recv_sem=ax_recv.at[turn, way, index],
+            send_sem=ax_send.at[way],
+            recv_sem=ax_recv.at[turn, index],
             device_id={"ax": ax + 1 if up else ax - 1},
         )
 
@@ -102,40 +116,37 @@
         def _():
             axial(field, turn, index, False).start()
 
-    def axial_wait(field, turn, index):
-        @pl.when(has_dn)
-        def _():
-            axial(field, turn, index, True).wait_recv()
-
-        @pl.when(has_up)
-        def _():
-            axial(field, turn, index, False).wait_recv()
-
-    def axial_drain(field, turn, index):
-        @pl.when(has_up)
-        def _():
-            axial(field, turn, index, True).wait_send()
-
-        @pl.when(has_dn)
-        def _():
-            axial(field, turn, index, False).wait_send()
+    def axial_wait(turn, index):
+        lanes = pl.ds(pl.multiple_of(index * CHUNK, LANE), CHUNK)
+
+        @pl.when(jnp.logical_and(has_up, has_dn))
+        def _():
+            all_of(out.at[:, 0:2, :, lanes], ax_recv.at[turn, index])
+
+        @pl.when(has_up != has_dn)
+        def _():
+            all_of(out.at[:, 0:1, :, lanes], ax_recv.at[turn, index])
 
     def sector(turn, way, part):
         where = (slice(None), slice(None), slice(None), pl.ds(pl.multiple_of(part * CHUNK, LANE), CHUNK))
         return pltpu.make_async_remote_copy(
             src_ref=t_send.at[(turn, way) + where],
             dst_ref=t_recv.at[(turn, way) + where],
-            send_sem=az_send.at[turn, way, part],
-            recv_sem=az_recv.at[turn, way, part],
+            send_sem=az_send.at[0],
+            recv_sem=az_recv.at[turn, part],
             device_id={"az": nxt if way == 0 else prv},
         )
+
+    def sector_wait(turn, part):
+        lanes = pl.ds(pl.multiple_of(part * CHUNK, LANE), CHUNK)
+        all_of(t_recv.at[turn, :, :, :, :, lanes], az_recv.at[turn, part])
 
     def spread(turn, d):
         return pltpu.make_async_remote_copy(
             src_ref=g_send.at[turn],
             dst_ref=g_recv[turn].at[d - d_min],
-            send_sem=ag_send.at[turn, d - d_min],
-            recv_sem=ag_recv.at[turn, d - d_min],
+            send_sem=ag_send.at[turn],
+            recv_sem=ag_recv.at[turn],
             device_id={"az": lax.rem(az + d, n_az)},
         )
 
@@ -228,22 +239,36 @@
             work(p, p, base, tbase)
 
     neighbours = has_up.astype(jnp.int32) + has_dn.astype(jnp.int32)
-    pl.semaphore_wait(barrier, neighbours + number_before([1, n_az - 1] + layer_peers))
-    for d, slot in [(n_az - 1, 0), (1, 1)] + [(d, 2) for d in layer_peers]:
-
-        @pl.when(before(d))
+
+    @pl.when(jnp.logical_not(first_even))
+    def _():
+        pl.semaphore_wait(barrier, neighbours + number_before([1, n_az - 1] + layer_peers))
+
+    signal_axial(ready.at[2], first_odd)
+    for d, slot in [(n_az - 1, 0), (1, 1)] + [(d, 3 + n_az - d - d_min) for d in layer_peers]:
+
+        @pl.when(jnp.logical_and(before(d), jnp.logical_not(direct(d))))
         def _(d=d, slot=slot):
             pl.semaphore_signal(ready.at[slot], inc=1, device_id={"az": sector_at(d)})
 
-    for copy in outer_loads:
-        copy.wait()
+    @pl.when(first_even)
+    def _():
+        pl.semaphore_wait(ready.at[2], neighbours)
+
+    loaded(2, 0)
     parts = range(count)
-    order = [edge, edge + 1] + list(range(edge)) + list(range(edge + 2, count))
+    order = [*range(edge), edge + 2, edge, edge + 1, *range(edge + 3, count)]
     for index in order:
         axial_start(q, 0, index)
 
-    for copy in inner_loads:
-        copy.wait()
+    loaded(planes - 2, 1)
+    pack_layers(q, 0)
+    for d in layer_peers:
+
+        @pl.when(before(d))
+        def _(d=d):
+            spread(0, d).start()
+
     for slot in range(planes):
         p = slot
         for v in range(nv):
@@ -264,13 +289,6 @@
     def _():
         sector_start(0)
 
-    pack_layers(q, 0)
-    for d in layer_peers:
-
-        @pl.when(before(d))
-        def _(d=d):
-            spread(0, d).start()
-
     @pl.when(jnp.logical_not(before(1)))
     def _():
         pl.semaphore_wait(ready.at[0], 1)
@@ -292,29 +310,33 @@
             for v in range(nv):
                 field[v, planes + 1, :, :] = jnp.zeros((cells, 2 * wide), jnp.float32)
 
-    @pl.when(jnp.logical_not(before(n_az - 1)))
-    def _():
-        pl.semaphore_wait(ready.at[1], 1)
-        sector_start(1)
-
-    after = len(layer_peers) - number_before(layer_peers)
-
-    @pl.when(after > 0)
-    def _():
-        pl.semaphore_wait(ready.at[2], after)
+    @pl.when(first_even)
+    def _():
+        pl.semaphore_wait(barrier, 1 + len(layer_peers))
 
     for d in layer_peers:
 
         @pl.when(jnp.logical_not(before(d)))
         def _(d=d):
+            @pl.when(jnp.logical_not(first_even))
+            def _():
+                pl.semaphore_wait(ready.at[3 + d - d_min], 1)
+
             spread(0, d).start()
+
+    @pl.when(first_odd)
+    def _():
+        pl.semaphore_wait(ready.at[1], 1)
+
+    @pl.when(az == 0)
+    def _():
+        sector_start(1)
 
     def run_first(low, high):
         @pl.loop(low, high)
         def _(index):
-            for way in range(2):
-                sector(0, way, index).wait_recv()
-            axial_wait(q, 0, index)
+            sector_wait(0, index)
+            axial_wait(0, index)
             evaluate_chunk(first, index, range(planes))
             axial_start(s, 1, index)
             for way in range(2):
@@ -323,40 +345,42 @@
     def run_second(low, high):
         @pl.loop(low, high)
         def _(index):
-            for way in range(2):
-                sector(1, way, index).wait_recv()
+            sector_wait(1, index)
             evaluate_chunk(second, index, range(1, planes - 1))
-            axial_wait(s, 1, index)
+            axial_wait(1, index)
             evaluate_chunk(second, index, (0, planes - 1))
 
-    for d in range(d_min, d_max + 1):
-        spread(0, d).wait_recv()
+    run_first(0, edge)
+    run_first(edge + 2, edge + 3)
+    split = jnp.where(az == n_az - 1, count, edge + 3)
+    run_first(edge + 3, split)
+    all_of(g_recv[0], ag_recv.at[0])
     for scalar in scalars:
         scalar.wait()
     unpack_ghosts(q, 0)
     run_first(edge, edge + 2)
     pack_layers(s, 1)
-    for d in range(d_min, d_max + 1):
+    for d in layer_peers:
         spread(1, d).start()
-    run_first(0, edge)
-    run_first(edge + 2, count)
+    run_first(split, count)
 
     run_second(0, edge)
-    run_second(edge + 2, count - 1)
-    for d in range(d_min, d_max + 1):
-        spread(1, d).wait_recv()
+    run_second(edge + 2, count)
+    all_of(g_recv[1], ag_recv.at[1])
     unpack_ghosts(s, 1)
     run_second(edge, edge + 2)
-    run_second(count - 1, count)
-
-    for turn, field in ((0, q), (1, s)):
-        for d in range(d_min, d_max + 1):
-            spread(turn, d).wait_send()
-        for part in parts:
-            for way in range(2):
-                sector(turn, way, part).wait_send()
-        for index in range(count):
-            axial_drain(field, turn, index)
+
+    for turn in range(2):
+        all_of(g_recv[turn], ag_send.at[turn])
+    all_of(t_send, az_send.at[0])
+
+    @pl.when(has_up)
+    def _():
+        all_of(out.at[:, 0:2], ax_send.at[0])
+
+    @pl.when(has_dn)
+    def _():
+        all_of(out.at[:, 0:2], ax_send.at[1])
 
 
 def shards(n_ax, n_az, state, rotor_offset, rotor_fraction):
@@ -387,14 +411,14 @@
             pltpu.VMEM((reach, cells, LANE), jnp.float32),
             pltpu.SMEM((1,), jnp.int32),
             pltpu.SMEM((1,), jnp.float32),
-            sem((4, 2)),
-            sem((2, 2, count)),
-            sem((2, 2, count)),
-            sem((2, 2, count)),
-            sem((2, 2, count)),
-            sem((2, reach)),
-            sem((2, reach)),
-            pltpu.SemaphoreType.REGULAR((3,)),
+            sem((4,)),
+            sem((2,)),
+            sem((2, count)),
+            sem((1,)),
+            sem((2, count)),
+            sem((2,)),
+            sem((2,)),
+            pltpu.SemaphoreType.REGULAR((3 + reach,)),
         ],
         compiler_params=pltpu.CompilerParams(collective_id=0, has_side_effects=True, vmem_limit_bytes=55_000_000),
     )(rotor_offset, rotor_fraction, state)

time: 23.7 us -> 19.8 us (0.84)
  Pallas kernels: 21.2 us -> 17.3 us
    pallas_call x1, Pallas kernels: 21.2 us -> 17.3 us  [shards(): pl.pallas_call(functools.partial(kernel, n_ax, n_az, d_min, d_max), out_s...]
where the time goes in v3:
time: 19.8 us; the launch traced here: 19.6 us
  Pallas kernels  17.3 us (87%)
  between operations  1.3 us (7%)
  local copies, waits for them, and re-layouts  0.97 us (5%)
    pallas_call x1, Pallas kernels, shards(): pl.pallas_call(functools.partial(kernel, n_ax, n_az, d_min, d_max), out_s...  17.3 us
    unnamed x1, local copies, waits for them, and re-layouts  0.97 us

profile of v3, /device:TPU:0, one launch (start us, length us, event | category | flops | bytes accessed | tf_op | source)
XLA Modules:
  0.0 19.6 jit_solution(16802832352823631593)
XLA Ops:
  1.3 17.3 %shard_map.37 = f32[4,4,8,2048]{3,2,1,0:T(8,128)S(1)} custom-call(s32[1]{0:T(128)S(6)} %copy.5.off_hbm, f32[1]{0:T(128)S(6)} %copy.6.frac_hbm, f32[4,4,8,2048]{3,2,1,0:T(8,128)} %state.1), custom_call_target="tpu_custom_call" | custom-call | tf_op jit(solution)/shard_map/pallas_call | solution.py:395
  18.6 1.0 %copy.7 = f32[4,4,8,2048]{3,2,1,0:T(8,128)} copy(f32[4,4,8,2048]{3,2,1,0:T(8,128)S(1)} %shard_map.37) | data formatting | bytes 2097152

commit v4 on v3

--- a/solution.py
+++ b/solution.py
@@ -14,11 +14,13 @@
 LANE = 128
 TILE = 256
 CHUNK = 256
-
-
-def kernel(n_ax, n_az, d_min, d_max, off_hbm, frac_hbm, state, out, q, s, t_send, t_recv, g_send, g_recv0, g_recv1,
-           off_ref, frac_ref, load_sem, ax_send, ax_recv, az_send, az_recv, ag_send, ag_recv, ready):
+GROUPS = 3
+
+
+def kernel(n_ax, n_az, d_min, d_max, off_ref, frac_ref, state, out, q, s, t_send, t_recv, g_send, g_recv0, g_recv1,
+           load_sem, ax_send, az_send, ag_send, halo_recv, ax_recv, az_recv, ag_recv, ready):
     nv, planes, cells, radial = state.shape
+    assert 2 * planes == cells
     half = radial // 2
     wide = half + 2 * LANE
     per_half = half // CHUNK
@@ -41,11 +43,7 @@
 
     outer_loads = [load(p, 1, h, 0) for p in (0, planes - 1) for h in range(2)]
     inner_loads = [load(1, planes - 2, h, 1) for h in range(2)]
-    scalars = [
-        pltpu.make_async_copy(off_hbm, off_ref, load_sem.at[2]),
-        pltpu.make_async_copy(frac_hbm, frac_ref, load_sem.at[3]),
-    ]
-    for copy in outer_loads + inner_loads + scalars:
+    for copy in outer_loads + inner_loads:
         copy.start()
 
     def all_of(ref, semaphore):
@@ -59,7 +57,11 @@
     layer_peers = list(range(d_min, d_max + 1))
     even = lax.rem(ax, 2) == 0
     first_even = jnp.logical_and(az == 0, even)
-    first_odd = jnp.logical_and(az == 0, jnp.logical_not(even))
+    odd = jnp.logical_not(even)
+    first_odd = jnp.logical_and(az == 0, odd)
+
+    def group_of(d):
+        return 3 + (d - d_min) * GROUPS // len(layer_peers)
 
     def sector_at(d):
         return lax.rem(az + d, n_az)
@@ -82,7 +84,7 @@
         def _():
             pl.semaphore_signal(semaphore, inc=1, device_id={"ax": ax - 1})
 
-    signal_axial(barrier, jnp.logical_not(first_odd))
+    signal_axial(barrier, even)
     for d in [1, n_az - 1] + layer_peers:
 
         @pl.when(jnp.logical_or(jnp.logical_not(before(d)), direct(d)))
@@ -103,7 +105,7 @@
             src_ref=field.at[:, planes if up else 1, :, lanes],
             dst_ref=field.at[:, 0 if up else planes + 1, :, lanes],
             send_sem=ax_send.at[way],
-            recv_sem=ax_recv.at[turn, index],
+            recv_sem=(ax_recv if turn else halo_recv).at[index],
             device_id={"ax": ax + 1 if up else ax - 1},
         )
 
@@ -116,16 +118,22 @@
         def _():
             axial(field, turn, index, False).start()
 
-    def axial_wait(turn, index):
+    def planes_wait(semaphore, index, more):
         lanes = pl.ds(pl.multiple_of(index * CHUNK, LANE), CHUNK)
 
         @pl.when(jnp.logical_and(has_up, has_dn))
         def _():
-            all_of(out.at[:, 0:2, :, lanes], ax_recv.at[turn, index])
+            all_of(out.at[:, 0 : 2 + more, :, lanes], semaphore.at[index])
 
         @pl.when(has_up != has_dn)
         def _():
-            all_of(out.at[:, 0:1, :, lanes], ax_recv.at[turn, index])
+            all_of(out.at[:, 0 : 1 + more, :, lanes], semaphore.at[index])
+
+        if more:
+
+            @pl.when(jnp.logical_not(jnp.logical_or(has_up, has_dn)))
+            def _():
+                all_of(out.at[:, 0:more, :, lanes], semaphore.at[index])
 
     def sector(turn, way, part):
         where = (slice(None), slice(None), slice(None), pl.ds(pl.multiple_of(part * CHUNK, LANE), CHUNK))
@@ -133,13 +141,13 @@
             src_ref=t_send.at[(turn, way) + where],
             dst_ref=t_recv.at[(turn, way) + where],
             send_sem=az_send.at[0],
-            recv_sem=az_recv.at[turn, part],
+            recv_sem=(az_recv if turn else halo_recv).at[part],
             device_id={"az": nxt if way == 0 else prv},
         )
 
-    def sector_wait(turn, part):
+    def sector_wait(part):
         lanes = pl.ds(pl.multiple_of(part * CHUNK, LANE), CHUNK)
-        all_of(t_recv.at[turn, :, :, :, :, lanes], az_recv.at[turn, part])
+        all_of(t_recv.at[1, :, :, :, :, lanes], az_recv.at[part])
 
     def spread(turn, d):
         return pltpu.make_async_remote_copy(
@@ -189,7 +197,8 @@
                 field[v, p + 1, :, wide : wide + LANE] = pltpu.roll(sta, LANE - 1 - other, 1)
 
     def evaluate(field, turn, p, slot, base, tbase):
-        values, grads, seconds = [], [], []
+        rates = [0.5 * step_size * field[v, p + 1, :, pl.ds(base + LANE, TILE)] for v in range(3)]
+        moved, seconds = [], []
         strain = None
         for v in range(nv):
             ext = field[v, p + 1, :, pl.ds(base, TILE + 2 * LANE)]
@@ -202,34 +211,25 @@
             after = t_recv[turn, 1, slot, v, :, pl.ds(tbase, TILE)]
             up_t = pltpu.roll(jnp.where(sub == 0, after, value), cells - 1, 0)
             dn_t = pltpu.roll(jnp.where(sub == cells - 1, before, value), 1, 0)
-            grad = ((up_p - dn_p) * 0.5, (up_t - dn_t) * 0.5, (up_r - dn_r) * 0.5)
-            second = (up_p + dn_p) + (up_t + dn_t) + (up_r + dn_r) - 6.0 * value
+            across = (up_p - dn_p, up_t - dn_t, up_r - dn_r)
+            seconds.append((up_p + dn_p) + (up_t + dn_t) + (up_r + dn_r) - 6.0 * value)
+            moved.append(value - (rates[0] * across[0] + rates[1] * across[1] + rates[2] * across[2]))
             if v < 3:
-                square = grad[0] * grad[0] + grad[1] * grad[1] + grad[2] * grad[2]
+                square = across[0] * across[0] + across[1] * across[1] + across[2] * across[2]
                 strain = square if strain is None else strain + square
-            values.append(value)
-            grads.append(grad)
-            seconds.append(second)
-        viscous = base_viscosity + eddy_coeff * jnp.sqrt(strain)
-        steps = []
-        for v in range(nv):
-            advect = values[0] * grads[v][0] + values[1] * grads[v][1] + values[2] * grads[v][2]
-            steps.append(step_size * (viscous * seconds[v] - advect))
-        return values, steps
+        viscous = step_size * base_viscosity + (0.5 * step_size * eddy_coeff) * jnp.sqrt(strain)
+        return [moved[v] + viscous * seconds[v] for v in range(nv)]
 
     def first(p, slot, base, tbase):
-        values, steps = evaluate(q, 0, p, slot, base, tbase)
-        for v in range(nv):
-            section = values[v] + steps[v]
+        for v, section in enumerate(evaluate(q, 0, p, slot, base, tbase)):
             s[v, p + 1, :, pl.ds(base + LANE, TILE)] = section
             t_send[1, 0, slot, v, :, pl.ds(tbase, TILE)] = section[cells - 1 :, :]
             t_send[1, 1, slot, v, :, pl.ds(tbase, TILE)] = section[0:1, :]
 
     def second(p, slot, base, tbase):
-        values, steps = evaluate(s, 1, p, slot, base, tbase)
-        for v in range(nv):
+        for v, stepped in enumerate(evaluate(s, 1, p, slot, base, tbase)):
             before = q[v, p + 1, :, pl.ds(base + LANE, TILE)]
-            out[v, p, :, pl.ds(tbase, TILE)] = 0.5 * (before + (values[v] + steps[v]))
+            out[v, p, :, pl.ds(tbase, TILE)] = 0.5 * (before + stepped)
 
     def evaluate_chunk(work, index, which):
         h, c = index // per_half, index % per_half
@@ -242,26 +242,50 @@
 
     @pl.when(jnp.logical_not(first_even))
     def _():
-        pl.semaphore_wait(barrier, neighbours + number_before([1, n_az - 1] + layer_peers))
-
-    signal_axial(ready.at[2], first_odd)
-    for d, slot in [(n_az - 1, 0), (1, 1)] + [(d, 3 + n_az - d - d_min) for d in layer_peers]:
+        pl.semaphore_wait(barrier, jnp.where(odd, neighbours, 0) + number_before([1, n_az - 1] + layer_peers))
+
+    signal_axial(ready.at[2], odd)
+    for d, slot in [(n_az - 1, 0), (1, 1)] + [(d, group_of(n_az - d)) for d in layer_peers]:
 
         @pl.when(jnp.logical_and(before(d), jnp.logical_not(direct(d))))
         def _(d=d, slot=slot):
             pl.semaphore_signal(ready.at[slot], inc=1, device_id={"az": sector_at(d)})
 
-    @pl.when(first_even)
-    def _():
-        pl.semaphore_wait(ready.at[2], neighbours)
-
     loaded(2, 0)
     parts = range(count)
-    order = [*range(edge), edge + 2, edge, edge + 1, *range(edge + 3, count)]
-    for index in order:
-        axial_start(q, 0, index)
+    last = jnp.logical_or(az == 0, az == n_az - 1)
+    others = [*range(edge), *range(edge + 2, count)]
+    order = [*others[: edge - 1], edge, edge + 1, *others[edge - 1 :]]
+    order_last = [*others, edge, edge + 1]
+
+    def planes_start():
+        for index, index_last in zip(order, order_last):
+            axial_start(q, 0, jnp.where(last, index_last, index))
+
+    @pl.when(odd)
+    def _():
+        planes_start()
 
     loaded(planes - 2, 1)
+
+    def pack_rows(way):
+        row = slice(0, 1) if way else slice(cells - 1, cells)
+        for p in range(planes):
+            for v in range(nv):
+                for h in range(2):
+                    lanes = slice(h * wide + LANE, h * wide + LANE + half)
+                    t_send[0, way, p, v, :, h * half : (h + 1) * half] = q[v, p + 1, row, lanes]
+
+    def sector_start(way):
+        to_last = az <= 1 if way else az >= n_az - 2
+        for index, index_last in zip(order, order_last):
+            sector(0, way, jnp.where(to_last, index_last, index)).start()
+
+    @pl.when(az == n_az - 1)
+    def _():
+        pack_rows(0)
+        sector_start(0)
+
     pack_layers(q, 0)
     for d in layer_peers:
 
@@ -269,25 +293,20 @@
         def _(d=d):
             spread(0, d).start()
 
-    for slot in range(planes):
-        p = slot
-        for v in range(nv):
-            for h in range(2):
-                lanes = slice(h * wide + LANE, h * wide + LANE + half)
-                t_send[0, 0, slot, v, :, h * half : (h + 1) * half] = q[v, p + 1, cells - 1 : cells, lanes]
-                t_send[0, 1, slot, v, :, h * half : (h + 1) * half] = q[v, p + 1, 0:1, lanes]
-
-    def sector_start(way):
-        for index in order:
-            sector(0, way, index).start()
-
-    @pl.when(before(n_az - 1))
+    @pl.when(az < n_az - 1)
+    def _():
+        pack_rows(0)
+
+    pack_rows(1)
+
+    @pl.when(az > 0)
     def _():
         sector_start(1)
 
-    @pl.when(before(1))
-    def _():
-        sector_start(0)
+    @pl.when(even)
+    def _():
+        pl.semaphore_wait(ready.at[2], neighbours)
+        planes_start()
 
     @pl.when(jnp.logical_not(before(1)))
     def _():
@@ -314,15 +333,19 @@
     def _():
         pl.semaphore_wait(barrier, 1 + len(layer_peers))
 
-    for d in layer_peers:
-
-        @pl.when(jnp.logical_not(before(d)))
-        def _(d=d):
-            @pl.when(jnp.logical_not(first_even))
-            def _():
-                pl.semaphore_wait(ready.at[3 + d - d_min], 1)
-
-            spread(0, d).start()
+    for group in range(3, 3 + GROUPS):
+        members = [d for d in layer_peers if group_of(d) == group]
+        after = len(members) - number_before(members)
+
+        @pl.when(jnp.logical_and(after > 0, jnp.logical_not(first_even)))
+        def _(group=group, after=after):
+            pl.semaphore_wait(ready.at[group], after)
+
+        for d in members:
+
+            @pl.when(jnp.logical_not(before(d)))
+            def _(d=d):
+                spread(0, d).start()
 
     @pl.when(first_odd)
     def _():
@@ -331,44 +354,66 @@
     @pl.when(az == 0)
     def _():
         sector_start(1)
+
+    def other(place):
+        return place + jnp.where(place < edge, 0, 2)
+
+    def first_chunk(index, send):
+        planes_wait(halo_recv, index, 1)
+        evaluate_chunk(first, index, range(planes))
+
+        @pl.when(send)
+        def _():
+            axial_start(s, 1, index)
+
+        for way in range(2):
+            sector(1, way, index).start()
+
+    def second_chunk(index):
+        sector_wait(index)
+        evaluate_chunk(second, index, range(1, planes - 1))
+        planes_wait(ax_recv, index, 0)
+        evaluate_chunk(second, index, (0, planes - 1))
 
     def run_first(low, high):
         @pl.loop(low, high)
-        def _(index):
-            sector_wait(0, index)
-            axial_wait(0, index)
-            evaluate_chunk(first, index, range(planes))
-            axial_start(s, 1, index)
-            for way in range(2):
-                sector(1, way, index).start()
+        def _(place):
+            first_chunk(other(place), jnp.logical_or(az != 1, place < edge - 1))
 
     def run_second(low, high):
         @pl.loop(low, high)
-        def _(index):
-            sector_wait(1, index)
-            evaluate_chunk(second, index, range(1, planes - 1))
-            axial_wait(1, index)
-            evaluate_chunk(second, index, (0, planes - 1))
-
-    run_first(0, edge)
-    run_first(edge + 2, edge + 3)
-    split = jnp.where(az == n_az - 1, count, edge + 3)
-    run_first(edge + 3, split)
+        def _(place):
+            second_chunk(other(place))
+
+            @pl.when(jnp.logical_and(az == 1, place == edge - 2))
+            def _():
+                for index in others[edge - 1 :]:
+                    axial_start(s, 1, index)
+
+    split = jnp.where(last, len(others), edge - 1)
+    run_first(0, split)
     all_of(g_recv[0], ag_recv.at[0])
-    for scalar in scalars:
-        scalar.wait()
     unpack_ghosts(q, 0)
-    run_first(edge, edge + 2)
+
+    @pl.loop(edge, edge + 2)
+    def _(index):
+        first_chunk(index, True)
+
     pack_layers(s, 1)
     for d in layer_peers:
         spread(1, d).start()
-    run_first(split, count)
-
-    run_second(0, edge)
-    run_second(edge + 2, count)
+    run_first(split, len(others))
+
+    split = jnp.where(last, len(others), jnp.where(2 * az < n_az, edge + 1, edge - 1))
+    run_second(0, split)
     all_of(g_recv[1], ag_recv.at[1])
     unpack_ghosts(s, 1)
-    run_second(edge, edge + 2)
+
+    @pl.loop(edge, edge + 2)
+    def _(index):
+        second_chunk(index)
+
+    run_second(split, len(others))
 
     for turn in range(2):
         all_of(g_recv[turn], ag_send.at[turn])
@@ -396,8 +441,8 @@
         functools.partial(kernel, n_ax, n_az, d_min, d_max),
         out_shape=jax.ShapeDtypeStruct(state.shape, state.dtype),
         in_specs=[
-            pl.BlockSpec(memory_space=pltpu.HBM),
-            pl.BlockSpec(memory_space=pltpu.HBM),
+            pl.BlockSpec(memory_space=pltpu.SMEM),
+            pl.BlockSpec(memory_space=pltpu.SMEM),
             pl.BlockSpec(memory_space=pltpu.HBM),
         ],
         out_specs=pl.BlockSpec(memory_space=pltpu.VMEM),
@@ -409,16 +454,15 @@
             pltpu.VMEM((2, cells, LANE), jnp.float32),
             pltpu.VMEM((reach, cells, LANE), jnp.float32),
             pltpu.VMEM((reach, cells, LANE), jnp.float32),
-            pltpu.SMEM((1,), jnp.int32),
-            pltpu.SMEM((1,), jnp.float32),
-            sem((4,)),
-            sem((2,)),
-            sem((2, count)),
-            sem((1,)),
-            sem((2, count)),
             sem((2,)),
             sem((2,)),
-            pltpu.SemaphoreType.REGULAR((3 + reach,)),
+            sem((1,)),
+            sem((2,)),
+            sem((count,)),
+            sem((count,)),
+            sem((count,)),
+            sem((2,)),
+            pltpu.SemaphoreType.REGULAR((3 + GROUPS,)),
         ],
         compiler_params=pltpu.CompilerParams(collective_id=0, has_side_effects=True, vmem_limit_bytes=55_000_000),
     )(rotor_offset, rotor_fraction, state)

time: 19.8 us -> 18.9 us (0.955)
  Pallas kernels: 17.3 us -> 16.3 us
    pallas_call x1, Pallas kernels: 17.3 us -> 16.3 us  [shards(): pl.pallas_call(functools.partial(kernel, n_ax, n_az, d_min, d_max), out_s...]
where the time goes in v4:
time: 18.9 us; the launch traced here: 18.6 us
  Pallas kernels  16.3 us (86%)
  between operations  1.3 us (7%)
  local copies, waits for them, and re-layouts  0.97 us (5%)
    pallas_call x1, Pallas kernels, shards(): pl.pallas_call(functools.partial(kernel, n_ax, n_az, d_min, d_max), out_s...  16.3 us
    unnamed x1, local copies, waits for them, and re-layouts  0.97 us

profile of v4, /device:TPU:0, one launch (start us, length us, event | category | flops | bytes accessed | tf_op | source)
XLA Modules:
  0.0 18.6 jit_solution(12395380164558829713)
XLA Ops:
  1.3 16.3 %shard_map.37 = f32[4,4,8,2048]{3,2,1,0:T(8,128)S(1)} custom-call(s32[1]{0:T(128)S(6)} %copy.5.off_ref, f32[1]{0:T(128)S(6)} %copy.6.frac_ref, f32[4,4,8,2048]{3,2,1,0:T(8,128)} %state.1), custom_call_target="tpu_custom_call" | custom-call | tf_op jit(solution)/shard_map/pallas_call | solution.py:440
  17.6 1.0 %copy.7 = f32[4,4,8,2048]{3,2,1,0:T(8,128)} copy(f32[4,4,8,2048]{3,2,1,0:T(8,128)S(1)} %shard_map.37) | data formatting | bytes 2097152

commit v5 on v4

--- a/solution.py
+++ b/solution.py
@@ -17,7 +17,7 @@
 GROUPS = 3
 
 
-def kernel(n_ax, n_az, d_min, d_max, off_ref, frac_ref, state, out, q, s, t_send, t_recv, g_send, g_recv0, g_recv1,
+def kernel(n_ax, n_az, d_min, d_max, off_ref, frac_ref, state, out, q, s, pre_r, pre_t, pre_b, t_send, t_recv, g_send, g_recv0, g_recv1,
            load_sem, ax_send, az_send, ag_send, halo_recv, ax_recv, az_recv, ag_recv, ready):
     nv, planes, cells, radial = state.shape
     assert 2 * planes == cells
@@ -172,7 +172,7 @@
                 packed = jnp.where(lane1 == other, pltpu.roll(rotor, other + 1, 1), packed)
         g_send[turn] = packed
 
-    def unpack_ghosts(field, turn):
+    def unpack_ghosts(turn):
         off = off_ref[0]
         f = frac_ref[0]
 
@@ -193,26 +193,44 @@
             for p in range(planes):
                 index = v * planes + p
                 other = nv * planes + index
-                field[v, p + 1, :, wide - LANE : wide] = pltpu.roll(rot, LANE - index, 1) if index else rot
-                field[v, p + 1, :, wide : wide + LANE] = pltpu.roll(sta, LANE - 1 - other, 1)
+                ghost = jnp.where(lane1 == LANE - 1, pltpu.roll(rot, LANE - 1 - index, 1), 0.0)
+                pre_r[v, p, :, half - LANE : half] += ghost
+                pre_b[v, p, :, half - LANE : half] += ghost
+                ghost = jnp.where(lane1 == 0, pltpu.roll(sta, LANE - other, 1), 0.0)
+                pre_r[v, p, :, half : half + LANE] -= ghost
+                pre_b[v, p, :, half : half + LANE] += ghost
+
+    def prepare(field):
+        @pl.loop(0, count)
+        def _(index):
+            h, c = index // per_half, index % per_half
+            base = pl.multiple_of(h * wide + c * CHUNK, LANE)
+            lanes = pl.ds(pl.multiple_of(index * CHUNK, LANE), TILE)
+            for p in range(planes):
+                for v in range(nv):
+                    ext = field[v, p + 1, :, pl.ds(base, TILE + 2 * LANE)]
+                    value = ext[:, LANE : LANE + TILE]
+                    up_r = pltpu.roll(ext, TILE + 2 * LANE - 1, 1)[:, LANE : LANE + TILE]
+                    dn_r = pltpu.roll(ext, 1, 1)[:, LANE : LANE + TILE]
+                    up_t = jnp.where(sub == cells - 1, 0.0, pltpu.roll(value, cells - 1, 0))
+                    dn_t = jnp.where(sub == 0, 0.0, pltpu.roll(value, 1, 0))
+                    pre_r[v, p, :, lanes] = up_r - dn_r
+                    pre_t[v, p, :, lanes] = up_t - dn_t
+                    pre_b[v, p, :, lanes] = (up_t + dn_t) + (up_r + dn_r) - 6.0 * value
 
     def evaluate(field, turn, p, slot, base, tbase):
         rates = [0.5 * step_size * field[v, p + 1, :, pl.ds(base + LANE, TILE)] for v in range(3)]
         moved, seconds = [], []
         strain = None
+        lanes = pl.ds(tbase, TILE)
         for v in range(nv):
-            ext = field[v, p + 1, :, pl.ds(base, TILE + 2 * LANE)]
-            value = ext[:, LANE : LANE + TILE]
-            up_r = pltpu.roll(ext, TILE + 2 * LANE - 1, 1)[:, LANE : LANE + TILE]
-            dn_r = pltpu.roll(ext, 1, 1)[:, LANE : LANE + TILE]
+            value = field[v, p + 1, :, pl.ds(base + LANE, TILE)]
             up_p = field[v, p + 2, :, pl.ds(base + LANE, TILE)]
             dn_p = field[v, p, :, pl.ds(base + LANE, TILE)]
-            before = t_recv[turn, 0, slot, v, :, pl.ds(tbase, TILE)]
-            after = t_recv[turn, 1, slot, v, :, pl.ds(tbase, TILE)]
-            up_t = pltpu.roll(jnp.where(sub == 0, after, value), cells - 1, 0)
-            dn_t = pltpu.roll(jnp.where(sub == cells - 1, before, value), 1, 0)
-            across = (up_p - dn_p, up_t - dn_t, up_r - dn_r)
-            seconds.append((up_p + dn_p) + (up_t + dn_t) + (up_r + dn_r) - 6.0 * value)
+            before = jnp.where(sub == 0, t_recv[turn, 0, slot, v, :, lanes], 0.0)
+            after = jnp.where(sub == cells - 1, t_recv[turn, 1, slot, v, :, lanes], 0.0)
+            across = (up_p - dn_p, pre_t[v, p, :, lanes] + (after - before), pre_r[v, p, :, lanes])
+            seconds.append((up_p + dn_p) + (after + before) + pre_b[v, p, :, lanes])
             moved.append(value - (rates[0] * across[0] + rates[1] * across[1] + rates[2] * across[2]))
             if v < 3:
                 square = across[0] * across[0] + across[1] * across[1] + across[2] * across[2]
@@ -317,6 +335,7 @@
         for v in range(nv):
             for p in range(planes):
                 field[v, p + 1, :, 0:LANE] = zero
+                field[v, p + 1, :, wide - LANE : wide + LANE] = jnp.zeros((cells, 2 * LANE), jnp.float32)
                 field[v, p + 1, :, 2 * wide - LANE :] = zero
 
         @pl.when(jnp.logical_not(has_dn))
@@ -328,6 +347,8 @@
         def _(field=field):
             for v in range(nv):
                 field[v, planes + 1, :, :] = jnp.zeros((cells, 2 * wide), jnp.float32)
+
+    prepare(q)
 
     @pl.when(first_even)
     def _():
@@ -393,7 +414,7 @@
     split = jnp.where(last, len(others), edge - 1)
     run_first(0, split)
     all_of(g_recv[0], ag_recv.at[0])
-    unpack_ghosts(q, 0)
+    unpack_ghosts(0)
 
     @pl.loop(edge, edge + 2)
     def _(index):
@@ -404,10 +425,11 @@
         spread(1, d).start()
     run_first(split, len(others))
 
+    prepare(s)
     split = jnp.where(last, len(others), jnp.where(2 * az < n_az, edge + 1, edge - 1))
     run_second(0, split)
     all_of(g_recv[1], ag_recv.at[1])
-    unpack_ghosts(s, 1)
+    unpack_ghosts(1)
 
     @pl.loop(edge, edge + 2)
     def _(index):
@@ -449,6 +471,9 @@
         scratch_shapes=[
             pltpu.VMEM((nv, planes + 2, cells, 2 * wide), jnp.float32),
             pltpu.VMEM((nv, planes + 2, cells, 2 * wide), jnp.float32),
+            pltpu.VMEM(state.shape, jnp.float32),
+            pltpu.VMEM(state.shape, jnp.float32),
+            pltpu.VMEM(state.shape, jnp.float32),
             pltpu.VMEM((2, 2, planes, nv, 1, radial), jnp.float32),
             pltpu.VMEM((2, 2, planes, nv, 1, radial), jnp.float32),
             pltpu.VMEM((2, cells, LANE), jnp.float32),

time: 18.9 us -> 18.5 us (0.979)
  Pallas kernels: 16.3 us -> 15.9 us
    pallas_call x1, Pallas kernels: 16.3 us -> 15.9 us  [shards(): pl.pallas_call(functools.partial(kernel, n_ax, n_az, d_min, d_max), out_s...]
where the time goes in v5:
time: 18.5 us; the launch traced here: 18.2 us
  Pallas kernels  15.9 us (86%)
  between operations  1.3 us (7%)
  local copies, waits for them, and re-layouts  0.97 us (5%)
    pallas_call x1, Pallas kernels, shards(): pl.pallas_call(functools.partial(kernel, n_ax, n_az, d_min, d_max), out_s...  15.9 us
    unnamed x1, local copies, waits for them, and re-layouts  0.97 us

profile of v5, /device:TPU:0, one launch (start us, length us, event | category | flops | bytes accessed | tf_op | source)
XLA Modules:
  0.0 18.2 jit_solution(14075791431185975393)
XLA Ops:
  1.3 15.9 %shard_map.37 = f32[4,4,8,2048]{3,2,1,0:T(8,128)S(1)} custom-call(s32[1]{0:T(128)S(6)} %copy.5.off_ref, f32[1]{0:T(128)S(6)} %copy.6.frac_ref, f32[4,4,8,2048]{3,2,1,0:T(8,128)} %state.1), custom_call_target="tpu_custom_call" | custom-call | tf_op jit(solution)/shard_map/pallas_call | solution.py:462
  17.2 1.0 %copy.7 = f32[4,4,8,2048]{3,2,1,0:T(8,128)} copy(f32[4,4,8,2048]{3,2,1,0:T(8,128)S(1)} %shard_map.37) | data formatting | bytes 2097152

commit v6 on v5

--- a/solution.py
+++ b/solution.py
@@ -18,9 +18,9 @@
 
 
 def kernel(n_ax, n_az, d_min, d_max, off_ref, frac_ref, state, out, q, s, pre_r, pre_t, pre_b, t_send, t_recv, g_send, g_recv0, g_recv1,
-           load_sem, ax_send, az_send, ag_send, halo_recv, ax_recv, az_recv, ag_recv, ready):
+           load_sem, halo_send, ag_send, halo_recv, ax_recv, az_recv, ag_recv, ready):
     nv, planes, cells, radial = state.shape
-    assert 2 * planes == cells
+    assert 2 * planes == cells and planes >= 4
     half = radial // 2
     wide = half + 2 * LANE
     per_half = half // CHUNK
@@ -41,10 +41,23 @@
             load_sem.at[slot],
         )
 
-    outer_loads = [load(p, 1, h, 0) for p in (0, planes - 1) for h in range(2)]
-    inner_loads = [load(1, planes - 2, h, 1) for h in range(2)]
-    for copy in outer_loads + inner_loads:
-        copy.start()
+    even = lax.rem(ax, 2) == 0
+    odd = jnp.logical_not(even)
+    bottom_loads = [load(0, 1, h, 0) for h in range(2)]
+    top_loads = [load(planes - 1, 1, h, 1) for h in range(2)]
+
+    @pl.when(even)
+    def _():
+        for copy in top_loads + bottom_loads:
+            copy.start()
+
+    @pl.when(odd)
+    def _():
+        for copy in bottom_loads + top_loads:
+            copy.start()
+
+    for h in range(2):
+        load(1, planes - 2, h, 2).start()
 
     def all_of(ref, semaphore):
         pltpu.make_async_copy(ref, ref, semaphore).wait()
@@ -55,13 +68,11 @@
     barrier = pltpu.get_barrier_semaphore()
 
     layer_peers = list(range(d_min, d_max + 1))
-    even = lax.rem(ax, 2) == 0
     first_even = jnp.logical_and(az == 0, even)
-    odd = jnp.logical_not(even)
     first_odd = jnp.logical_and(az == 0, odd)
 
     def group_of(d):
-        return 3 + (d - d_min) * GROUPS // len(layer_peers)
+        return 2 + (d - d_min) * GROUPS // len(layer_peers)
 
     def sector_at(d):
         return lax.rem(az + d, n_az)
@@ -104,7 +115,7 @@
         return pltpu.make_async_remote_copy(
             src_ref=field.at[:, planes if up else 1, :, lanes],
             dst_ref=field.at[:, 0 if up else planes + 1, :, lanes],
-            send_sem=ax_send.at[way],
+            send_sem=halo_send.at[0],
             recv_sem=(ax_recv if turn else halo_recv).at[index],
             device_id={"ax": ax + 1 if up else ax - 1},
         )
@@ -140,7 +151,7 @@
         return pltpu.make_async_remote_copy(
             src_ref=t_send.at[(turn, way) + where],
             dst_ref=t_recv.at[(turn, way) + where],
-            send_sem=az_send.at[0],
+            send_sem=halo_send.at[0],
             recv_sem=(az_recv if turn else halo_recv).at[part],
             device_id={"az": nxt if way == 0 else prv},
         )
@@ -200,8 +211,8 @@
                 pre_r[v, p, :, half : half + LANE] -= ghost
                 pre_b[v, p, :, half : half + LANE] += ghost
 
-    def prepare(field):
-        @pl.loop(0, count)
+    def prepare(field, low=0, high=count):
+        @pl.loop(low, high)
         def _(index):
             h, c = index // per_half, index % per_half
             base = pl.multiple_of(h * wide + c * CHUNK, LANE)
@@ -262,14 +273,13 @@
     def _():
         pl.semaphore_wait(barrier, jnp.where(odd, neighbours, 0) + number_before([1, n_az - 1] + layer_peers))
 
-    signal_axial(ready.at[2], odd)
+    signal_axial(ready.at[1], odd)
     for d, slot in [(n_az - 1, 0), (1, 1)] + [(d, group_of(n_az - d)) for d in layer_peers]:
 
         @pl.when(jnp.logical_and(before(d), jnp.logical_not(direct(d))))
         def _(d=d, slot=slot):
             pl.semaphore_signal(ready.at[slot], inc=1, device_id={"az": sector_at(d)})
 
-    loaded(2, 0)
     parts = range(count)
     last = jnp.logical_or(az == 0, az == n_az - 1)
     others = [*range(edge), *range(edge + 2, count)]
@@ -282,9 +292,26 @@
 
     @pl.when(odd)
     def _():
+        @pl.when(has_up)
+        def _():
+            loaded(1, 1)
+
+        @pl.when(has_dn)
+        def _():
+            loaded(1, 0)
+
         planes_start()
 
-    loaded(planes - 2, 1)
+    loaded(planes - 2, 2)
+
+    @pl.when(jnp.logical_or(even, jnp.logical_not(has_up)))
+    def _():
+        loaded(1, 1)
+
+    @pl.when(jnp.logical_or(even, jnp.logical_not(has_dn)))
+    def _():
+        loaded(1, 0)
+
 
     def pack_rows(way):
         row = slice(0, 1) if way else slice(cells - 1, cells)
@@ -323,7 +350,7 @@
 
     @pl.when(even)
     def _():
-        pl.semaphore_wait(ready.at[2], neighbours)
+        pl.semaphore_wait(ready.at[1], neighbours)
         planes_start()
 
     @pl.when(jnp.logical_not(before(1)))
@@ -348,13 +375,14 @@
             for v in range(nv):
                 field[v, planes + 1, :, :] = jnp.zeros((cells, 2 * wide), jnp.float32)
 
-    prepare(q)
+    early = jnp.where(2 * az < n_az - 2, count, 0)
+    prepare(q, 0, early)
 
     @pl.when(first_even)
     def _():
         pl.semaphore_wait(barrier, 1 + len(layer_peers))
 
-    for group in range(3, 3 + GROUPS):
+    for group in range(2, 2 + GROUPS):
         members = [d for d in layer_peers if group_of(d) == group]
         after = len(members) - number_before(members)
 
@@ -375,6 +403,8 @@
     @pl.when(az == 0)
     def _():
         sector_start(1)
+
+    prepare(q, early, count)
 
     def other(place):
         return place + jnp.where(place < edge, 0, 2)
@@ -426,7 +456,7 @@
     run_first(split, len(others))
 
     prepare(s)
-    split = jnp.where(last, len(others), jnp.where(2 * az < n_az, edge + 1, edge - 1))
+    split = jnp.where(last, len(others), jnp.where(az == 1, edge, jnp.where(2 * az < n_az, edge + 1, edge - 1)))
     run_second(0, split)
     all_of(g_recv[1], ag_recv.at[1])
     unpack_ghosts(1)
@@ -439,15 +469,18 @@
 
     for turn in range(2):
         all_of(g_recv[turn], ag_send.at[turn])
-    all_of(t_send, az_send.at[0])
-
-    @pl.when(has_up)
-    def _():
-        all_of(out.at[:, 0:2], ax_send.at[0])
-
-    @pl.when(has_dn)
-    def _():
-        all_of(out.at[:, 0:2], ax_send.at[1])
+
+    @pl.when(jnp.logical_and(has_up, has_dn))
+    def _():
+        all_of(q.at[:, 0:6, :, 0:radial], halo_send.at[0])
+
+    @pl.when(has_up != has_dn)
+    def _():
+        all_of(q.at[:, 0:4, :, 0:radial], halo_send.at[0])
+
+    @pl.when(jnp.logical_not(jnp.logical_or(has_up, has_dn)))
+    def _():
+        all_of(q.at[:, 0:2, :, 0:radial], halo_send.at[0])
 
 
 def shards(n_ax, n_az, state, rotor_offset, rotor_fraction):
@@ -479,15 +512,14 @@
             pltpu.VMEM((2, cells, LANE), jnp.float32),
             pltpu.VMEM((reach, cells, LANE), jnp.float32),
             pltpu.VMEM((reach, cells, LANE), jnp.float32),
-            sem((2,)),
-            sem((2,)),
+            sem((3,)),
             sem((1,)),
             sem((2,)),
             sem((count,)),
             sem((count,)),
             sem((count,)),
             sem((2,)),
-            pltpu.SemaphoreType.REGULAR((3 + GROUPS,)),
+            pltpu.SemaphoreType.REGULAR((2 + GROUPS,)),
         ],
         compiler_params=pltpu.CompilerParams(collective_id=0, has_side_effects=True, vmem_limit_bytes=55_000_000),
     )(rotor_offset, rotor_fraction, state)

time: 18.5 us -> 18.4 us (level)
  no operation moved by 1% of the time
where the time goes in v6:
time: 18.4 us; the launch traced here: 18.1 us
  Pallas kernels  15.8 us (86%)
  between operations  1.3 us (7%)
  local copies, waits for them, and re-layouts  0.97 us (5%)
    pallas_call x1, Pallas kernels, shards(): pl.pallas_call(functools.partial(kernel, n_ax, n_az, d_min, d_max), out_s...  15.8 us
    unnamed x1, local copies, waits for them, and re-layouts  0.97 us

profile of v6, /device:TPU:0, one launch (start us, length us, event | category | flops | bytes accessed | tf_op | source)
XLA Modules:
  0.0 18.1 jit_solution(1441030745904569113)
XLA Ops:
  1.3 15.8 %shard_map.37 = f32[4,4,8,2048]{3,2,1,0:T(8,128)S(1)} custom-call(s32[1]{0:T(128)S(6)} %copy.5.off_ref, f32[1]{0:T(128)S(6)} %copy.6.frac_ref, f32[4,4,8,2048]{3,2,1,0:T(8,128)} %state.1), custom_call_target="tpu_custom_call" | custom-call | tf_op jit(solution)/shard_map/pallas_call | solution.py:495
  17.1 1.0 %copy.7 = f32[4,4,8,2048]{3,2,1,0:T(8,128)} copy(f32[4,4,8,2048]{3,2,1,0:T(8,128)S(1)} %shard_map.37) | data formatting | bytes 2097152

commit v7 on v6

--- a/solution.py
+++ b/solution.py
@@ -18,7 +18,7 @@
 
 
 def kernel(n_ax, n_az, d_min, d_max, off_ref, frac_ref, state, out, q, s, pre_r, pre_t, pre_b, t_send, t_recv, g_send, g_recv0, g_recv1,
-           load_sem, halo_send, ag_send, halo_recv, ax_recv, az_recv, ag_recv, ready):
+           load_sem, halo_send, ag_send, halo_recv, ag_recv, ready):
     nv, planes, cells, radial = state.shape
     assert 2 * planes == cells and planes >= 4
     half = radial // 2
@@ -116,7 +116,7 @@
             src_ref=field.at[:, planes if up else 1, :, lanes],
             dst_ref=field.at[:, 0 if up else planes + 1, :, lanes],
             send_sem=halo_send.at[0],
-            recv_sem=(ax_recv if turn else halo_recv).at[index],
+            recv_sem=halo_recv.at[turn, index],
             device_id={"ax": ax + 1 if up else ax - 1},
         )
 
@@ -129,22 +129,20 @@
         def _():
             axial(field, turn, index, False).start()
 
-    def planes_wait(semaphore, index, more):
+    def halo_wait(turn, index):
         lanes = pl.ds(pl.multiple_of(index * CHUNK, LANE), CHUNK)
 
         @pl.when(jnp.logical_and(has_up, has_dn))
         def _():
-            all_of(out.at[:, 0 : 2 + more, :, lanes], semaphore.at[index])
+            all_of(out.at[:, 0:3, :, lanes], halo_recv.at[turn, index])
 
         @pl.when(has_up != has_dn)
         def _():
-            all_of(out.at[:, 0 : 1 + more, :, lanes], semaphore.at[index])
-
-        if more:
-
-            @pl.when(jnp.logical_not(jnp.logical_or(has_up, has_dn)))
-            def _():
-                all_of(out.at[:, 0:more, :, lanes], semaphore.at[index])
+            all_of(out.at[:, 0:2, :, lanes], halo_recv.at[turn, index])
+
+        @pl.when(jnp.logical_not(jnp.logical_or(has_up, has_dn)))
+        def _():
+            all_of(out.at[:, 0:1, :, lanes], halo_recv.at[turn, index])
 
     def sector(turn, way, part):
         where = (slice(None), slice(None), slice(None), pl.ds(pl.multiple_of(part * CHUNK, LANE), CHUNK))
@@ -152,13 +150,9 @@
             src_ref=t_send.at[(turn, way) + where],
             dst_ref=t_recv.at[(turn, way) + where],
             send_sem=halo_send.at[0],
-            recv_sem=(az_recv if turn else halo_recv).at[part],
+            recv_sem=halo_recv.at[turn, part],
             device_id={"az": nxt if way == 0 else prv},
         )
-
-    def sector_wait(part):
-        lanes = pl.ds(pl.multiple_of(part * CHUNK, LANE), CHUNK)
-        all_of(t_recv.at[1, :, :, :, :, lanes], az_recv.at[part])
 
     def spread(turn, d):
         return pltpu.make_async_remote_copy(
@@ -260,11 +254,11 @@
             before = q[v, p + 1, :, pl.ds(base + LANE, TILE)]
             out[v, p, :, pl.ds(tbase, TILE)] = 0.5 * (before + stepped)
 
-    def evaluate_chunk(work, index, which):
+    def evaluate_chunk(work, index):
         h, c = index // per_half, index % per_half
         base = pl.multiple_of(h * wide + c * CHUNK, LANE)
         tbase = pl.multiple_of(index * CHUNK, LANE)
-        for p in which:
+        for p in range(planes):
             work(p, p, base, tbase)
 
     neighbours = has_up.astype(jnp.int32) + has_dn.astype(jnp.int32)
@@ -410,8 +404,8 @@
         return place + jnp.where(place < edge, 0, 2)
 
     def first_chunk(index, send):
-        planes_wait(halo_recv, index, 1)
-        evaluate_chunk(first, index, range(planes))
+        halo_wait(0, index)
+        evaluate_chunk(first, index)
 
         @pl.when(send)
         def _():
@@ -421,10 +415,8 @@
             sector(1, way, index).start()
 
     def second_chunk(index):
-        sector_wait(index)
-        evaluate_chunk(second, index, range(1, planes - 1))
-        planes_wait(ax_recv, index, 0)
-        evaluate_chunk(second, index, (0, planes - 1))
+        halo_wait(1, index)
+        evaluate_chunk(second, index)
 
     def run_first(low, high):
         @pl.loop(low, high)
@@ -515,9 +507,7 @@
             sem((3,)),
             sem((1,)),
             sem((2,)),
-            sem((count,)),
-            sem((count,)),
-            sem((count,)),
+            sem((2, count)),
             sem((2,)),
             pltpu.SemaphoreType.REGULAR((2 + GROUPS,)),
         ],

time: 18.4 us -> 18.3 us (level)
  no operation moved by 1% of the time
where the time goes in v7:
time: 18.3 us; the launch traced here: 18 us
  Pallas kernels  15.7 us (86%)
  between operations  1.3 us (7%)
  local copies, waits for them, and re-layouts  0.97 us (5%)
    pallas_call x1, Pallas kernels, shards(): pl.pallas_call(functools.partial(kernel, n_ax, n_az, d_min, d_max), out_s...  15.7 us
    unnamed x1, local copies, waits for them, and re-layouts  0.97 us

profile of v7, /device:TPU:0, one launch (start us, length us, event | category | flops | bytes accessed | tf_op | source)
XLA Modules:
  0.0 18.0 jit_solution(14835299630455781650)
XLA Ops:
  1.3 15.7 %shard_map.37 = f32[4,4,8,2048]{3,2,1,0:T(8,128)S(1)} custom-call(s32[1]{0:T(128)S(6)} %copy.5.off_ref, f32[1]{0:T(128)S(6)} %copy.6.frac_ref, f32[4,4,8,2048]{3,2,1,0:T(8,128)} %state.1), custom_call_target="tpu_custom_call" | custom-call | tf_op jit(solution)/shard_map/pallas_call | solution.py:487
  17.1 1.0 %copy.7 = f32[4,4,8,2048]{3,2,1,0:T(8,128)} copy(f32[4,4,8,2048]{3,2,1,0:T(8,128)S(1)} %shard_map.37) | data formatting | bytes 2097152

commit v8 on v7

--- a/solution.py
+++ b/solution.py
@@ -426,12 +426,12 @@
     def run_second(low, high):
         @pl.loop(low, high)
         def _(place):
-            second_chunk(other(place))
-
             @pl.when(jnp.logical_and(az == 1, place == edge - 2))
             def _():
                 for index in others[edge - 1 :]:
                     axial_start(s, 1, index)
+
+            second_chunk(other(place))
 
     split = jnp.where(last, len(others), edge - 1)
     run_first(0, split)

time: 18.3 us -> 18.3 us (level)
  no operation moved by 1% of the time
where the time goes in v8:
time: 18.3 us; the launch traced here: 18 us
  Pallas kernels  15.7 us (86%)
  between operations  1.3 us (7%)
  local copies, waits for them, and re-layouts  0.97 us (5%)
    pallas_call x1, Pallas kernels, shards(): pl.pallas_call(functools.partial(kernel, n_ax, n_az, d_min, d_max), out_s...  15.7 us
    unnamed x1, local copies, waits for them, and re-layouts  0.97 us

profile of v8, /device:TPU:0, one launch (start us, length us, event | category | flops | bytes accessed | tf_op | source)
XLA Modules:
  0.0 18.0 jit_solution(1833702673757830394)
XLA Ops:
  1.3 15.7 %shard_map.37 = f32[4,4,8,2048]{3,2,1,0:T(8,128)S(1)} custom-call(s32[1]{0:T(128)S(6)} %copy.5.off_ref, f32[1]{0:T(128)S(6)} %copy.6.frac_ref, f32[4,4,8,2048]{3,2,1,0:T(8,128)} %state.1), custom_call_target="tpu_custom_call" | custom-call | tf_op jit(solution)/shard_map/pallas_call | solution.py:487
  17.1 1.0 %copy.7 = f32[4,4,8,2048]{3,2,1,0:T(8,128)} copy(f32[4,4,8,2048]{3,2,1,0:T(8,128)S(1)} %shard_map.37) | data formatting | bytes 2097152
